TPU v7x, 32 devices: a whole 2x2x4 slice. The times are simulated.
32 devices in a mesh: narrow: 4 (over x, core), wide: 8 (over z, y).
Axes of the slice: x: 2, y: 2, z: 4, core: 2. Of those that a mesh axis runs over, the one named last changes fastest.
Arguments:
- block_ids: int32 [512, 4], P(('narrow', 'wide')), may hold values from 0 to 511, as said below
- incidence: int32 [512, 4, 128, 128], P(('narrow', 'wide')), may hold values from 0 to 1
- costs: int32 [512, 128], P(('narrow', 'wide')), may hold values from 16 to 80
- start_mult: float32 [512, 128], replicated, may hold values from 0.25 to 4
- upper: float32 [1], replicated, may hold values from 65536 to 131072
Outputs:
- multipliers: float32 [512, 128], replicated
- primal_mean: float32 [512, 128], P(('narrow', 'wide'))
Inputs may be any that keep to these rules, and one draw needn't show every extreme that they name: `block_ids`: the 4 row blocks listed for one tile are distinct.
All inputs are finite; a program needn't handle non-finite values.
Results may differ from a plain program's by a relative error of at most 0.0003.
Values sent between devices are 32-bit elements; how exact they have to be, the bound alone decides.
A program may use at most 64 MiB of HBM per device.

v0:
```python
import jax
import jax.numpy as jnp
from jax import lax
from jax.sharding import PartitionSpec as P

BLK = 128
K = 4
ITERS = 3


def local(block_ids, incidence, costs, start_mult, upper):
    hi = lax.Precision.HIGHEST
    tiles_here = block_ids.shape[0]
    blocks = start_mult.shape[0]
    incf = incidence.astype(jnp.float32)
    costf = costs.astype(jnp.float32)
    onehot = (
        block_ids.reshape(tiles_here * K, 1) == jnp.arange(blocks, dtype=jnp.int32)[None, :]
    ).astype(jnp.float32)
    count_narrow = lax.axis_size("narrow")
    count_wide = lax.axis_size("wide")
    share_rows = blocks // lax.axis_size(("narrow", "wide"))
    share_start = lax.axis_index(("narrow", "wide")) * share_rows
    mult = start_mult
    primal_mean = jnp.zeros(costs.shape, jnp.float32)
    for step in range(ITERS):
        u_tile = jnp.take(mult, block_ids, axis=0)
        reduced = costf - jnp.einsum("tkrc,tkr->tc", incf, u_tile, precision=hi)
        primal = 1.0 / (1.0 + jnp.exp(reduced / 8.0))
        local_soft = jnp.sum(-8.0 * jax.nn.softplus(-reduced / 8.0))
        if step == 0:
            primal_mean = primal
        else:
            primal_mean = 0.3 * primal + 0.7 * primal_mean
        part = jnp.einsum("tkrc,tc->tkr", incf, primal_mean, precision=hi).reshape(
            tiles_here * K, BLK
        )
        row_part = jnp.dot(onehot.T, part, precision=hi, preferred_element_type=jnp.float32)
        outgoing = row_part.reshape(count_narrow, count_wide, share_rows, BLK)
        incoming = lax.all_to_all(
            lax.all_to_all(outgoing, "narrow", split_axis=0, concat_axis=0, tiled=True),
            "wide",
            split_axis=1,
            concat_axis=1,
            tiled=True,
        )
        cover_share = jnp.sum(jnp.sum(incoming, axis=0), axis=0)
        mult_share = lax.dynamic_slice_in_dim(mult, share_start, share_rows, 0)
        slope = 1.0 - cover_share
        norm, mult_total, late_sum = lax.psum(
            (jnp.sum(slope * slope), jnp.sum(mult_share), local_soft), ("narrow", "wide")
        )
        value = mult_total + late_sum
        size = (upper[0] - value) / (norm + 1e-06)
        new_share = jnp.maximum(0.0, mult_share + size * slope)
        mult = lax.all_gather(new_share, ("narrow", "wide"), axis=0, tiled=True)
    return (mult, primal_mean)


def solution(mesh):
    in_specs = (
        P(("narrow", "wide"), None),
        P(("narrow", "wide"), None, None, None),
        P(("narrow", "wide"), None),
        P(),
        P(),
    )
    out_specs = (P(), P(("narrow", "wide"), None))
    return jax.shard_map(local, mesh=mesh, in_specs=in_specs, out_specs=out_specs, check_vma=False)
```

profile of v0, /device:TPU:0, one launch (start us, length us, event | category | flops | bytes accessed | tf_op | source)
XLA Modules:
  0.0 426.2 jit_solution(1178383881923371404)
XLA Ops:
  0.6 0.7 compare_and_fusion
  1.3 0.7 compare_select_fusion.3
  2.0 0.8 copy.23
  3.2 1.5 gather_fusion
  4.8 4.1 fusion.10
  9.6 3.4 fusion.8
  13.3 10.0 %all_to_all.30 = f32[4,8,16,128]{3,2,1,0:T(8,128)S(1)} all-to-all(f32[4,8,16,128]{3,2,1,0:T(8,128)S(1)} %fusion.16), channel_id=1, replica_groups=mesh['narrow'=4,'wide'=8] {'narrow'}, dimensions={0} | all-to-all | bytes 524288 | tf_op jit(solution)/shard_map/all_to_all | solution.py:41
  23.3 0.7 copy.24
  24.1 5.8 %all-to-all-start.1 = ((f32[4,8,16,128]{3,2,0,1:T(8,128)}), f32[4,8,16,128]{3,2,0,1:T(8,128)S(1)}, u32[]{:S(2)}, u32[]{:S(2)}) async-start(f32[4,8,16,128]{3,2,0,1:T(8,128)} %copy.24), calls=%async_computation.1 | async-start | bytes 524288 | tf_op jit(solution)/shard_map/all_to_all | solution.py:40
  29.9 1.4 dynamic-slice_reduce_fusion.2
  32.6 5.8 %all-to-all-done.1 = f32[4,8,16,128]{3,2,0,1:T(8,128)S(1)} async-done(((f32[4,8,16,128]{3,2,0,1:T(8,128)}), f32[4,8,16,128]{3,2,0,1:T(8,128)S(1)}, u32[]{:S(2)}, u32[]{:S(2)}) %all-to-all-start.1) | async-done | bytes 262176 | tf_op jit(solution)/shard_map/all_to_all | solution.py:40
  39.7 39.0 %all-reduce.2 = (f32[]{:T(128)}, f32[]{:T(128)}) all-reduce(f32[]{:T(128)S(6)} %add.95, f32[]{:T(128)} %multiply_reduce_fusion.2), channel_id=1, replica_groups=mesh['narrow'=4,'wide'=8] {'narrow','wide'}, use_global_device_ids=true, to_apply=%region_1.2 | all-reduce | flops 2 | bytes 16 | tf_op jit(solution)/shard_map/psum | solution.py:50
  80.1 0.7 add_maximum_fusion.2
  80.8 67.3 %all_gather.9 = f32[512,128]{1,0:T(8,128)S(1)} all-gather(f32[16,128]{1,0:T(8,128)S(1)} %add_maximum_fusion.2), channel_id=1, replica_groups=mesh['narrow'=4,'wide'=8] {'narrow','wide'}, dimensions={0}, use_global_device_ids=true | all-gather | bytes 270336 | tf_op jit(solution)/shard_map/all_gather | solution.py:56
  148.8 4.1 fusion.6
  153.5 3.4 fusion.4
  157.3 8.4 %all_to_all.31 = f32[4,8,16,128]{3,2,1,0:T(8,128)S(1)} all-to-all(f32[4,8,16,128]{3,2,1,0:T(8,128)S(1)} %fusion.14), channel_id=1, replica_groups=mesh['narrow'=4,'wide'=8] {'narrow'}, dimensions={0} | all-to-all | bytes 524288 | tf_op jit(solution)/shard_map/all_to_all | solution.py:41
  165.7 0.7 copy.27
  166.4 3.4 all-to-all-start.3
  171.6 7.0 %all-to-all-done.3 = f32[4,8,16,128]{3,2,0,1:T(8,128)S(1)} async-done(((f32[4,8,16,128]{3,2,0,1:T(8,128)}), f32[4,8,16,128]{3,2,0,1:T(8,128)S(1)}, u32[]{:S(2)}, u32[]{:S(2)}) %all-to-all-start.3) | async-done | bytes 262176 | tf_op jit(solution)/shard_map/all_to_all | solution.py:40
  179.2 38.9 %all-reduce.1 = (f32[]{:T(128)}, f32[]{:T(128)}) all-reduce(f32[]{:T(128)S(6)} %add.100, f32[]{:T(128)} %multiply_reduce_fusion.1), channel_id=1, replica_groups=mesh['narrow'=4,'wide'=8] {'narrow','wide'}, use_global_device_ids=true, to_apply=%region_8.10 | all-reduce | flops 2 | bytes 16 | tf_op jit(solution)/shard_map/psum | solution.py:50
  219.5 67.5 %all_gather.10 = f32[512,128]{1,0:T(8,128)S(1)} all-gather(f32[16,128]{1,0:T(8,128)S(1)} %add_maximum_fusion.1), channel_id=1, replica_groups=mesh['narrow'=4,'wide'=8] {'narrow','wide'}, dimensions={0}, use_global_device_ids=true | all-gather | bytes 270336 | tf_op jit(solution)/shard_map/all_gather | solution.py:56
  287.6 4.1 fusion.2
  292.4 3.4 fusion
  296.1 8.4 %all_to_all.32 = f32[4,8,16,128]{3,2,1,0:T(8,128)S(1)} all-to-all(f32[4,8,16,128]{3,2,1,0:T(8,128)S(1)} %fusion.12), channel_id=1, replica_groups=mesh['narrow'=4,'wide'=8] {'narrow'}, dimensions={0} | all-to-all | bytes 524288 | tf_op jit(solution)/shard_map/all_to_all | solution.py:41
  304.5 0.7 copy.30
  305.2 3.4 all-to-all-start.5
  308.7 0.6 dynamic-slice_reduce_fusion
  310.5 6.9 %all-to-all-done.5 = f32[4,8,16,128]{3,2,0,1:T(8,128)S(1)} async-done(((f32[4,8,16,128]{3,2,0,1:T(8,128)}), f32[4,8,16,128]{3,2,0,1:T(8,128)S(1)}, u32[]{:S(2)}, u32[]{:S(2)}) %all-to-all-start.5) | async-done | bytes 262176 | tf_op jit(solution)/shard_map/all_to_all | solution.py:40
  318.1 38.9 %all-reduce = (f32[]{:T(128)}, f32[]{:T(128)}) all-reduce(f32[]{:T(128)S(6)} %add.106, f32[]{:T(128)} %multiply_reduce_fusion), channel_id=1, replica_groups=mesh['narrow'=4,'wide'=8] {'narrow','wide'}, use_global_device_ids=true, to_apply=%region_15.17 | all-reduce | flops 2 | bytes 16 | tf_op jit(solution)/shard_map/psum | solution.py:50
  358.2 67.3 %all_gather.11 = f32[512,128]{1,0:T(8,128)S(1)} all-gather(f32[16,128]{1,0:T(8,128)S(1)} %add_maximum_fusion), channel_id=1, replica_groups=mesh['narrow'=4,'wide'=8] {'narrow','wide'}, dimensions={0}, use_global_device_ids=true | all-gather | bytes 270336 | tf_op jit(solution)/shard_map/all_gather | solution.py:56
  425.5 0.7 copy.48
  (36 shorter events, 7.3 us)
Async XLA Ops:
  0.6 8.3 %copy-start.3 = (s32[16,128]{1,0:T(8,128)S(1)}, s32[16,128]{1,0:T(8,128)}, u32[]{:S(2)}) copy-start(s32[16,128]{1,0:T(8,128)} %param.9) | copy-start | bytes 24580
  4.7 4.9 %copy-start = (s32[16,4,128,128]{3,2,1,0:T(8,128)S(1)}, s32[16,4,128,128]{3,2,1,0:T(8,128)}, u32[]{:S(2)}) copy-start(s32[16,4,128,128]{3,2,1,0:T(8,128)} %param.8) | copy-start | bytes 12582916
  24.1 14.4 %all-to-all-start.1 = ((f32[4,8,16,128]{3,2,0,1:T(8,128)}), f32[4,8,16,128]{3,2,0,1:T(8,128)S(1)}, u32[]{:S(2)}, u32[]{:S(2)}) async-start(f32[4,8,16,128]{3,2,0,1:T(8,128)} %copy.24), calls=%async_computation.1 | async-start | bytes 524288 | tf_op jit(solution)/shard_map/all_to_all | solution.py:40
  148.7 4.8 %copy-start.1 = (s32[16,4,128,128]{3,2,1,0:T(8,128)S(1)}, s32[16,4,128,128]{3,2,1,0:T(8,128)}, u32[]{:S(2)}) copy-start(s32[16,4,128,128]{3,2,1,0:T(8,128)} %param.8) | copy-start | bytes 12582916
  166.4 12.2 %all-to-all-start.3 = ((f32[4,8,16,128]{3,2,0,1:T(8,128)}), f32[4,8,16,128]{3,2,0,1:T(8,128)S(1)}, u32[]{:S(2)}, u32[]{:S(2)}) async-start(f32[4,8,16,128]{3,2,0,1:T(8,128)} %copy.27), calls=%async_computation.3 | async-start | bytes 524288 | tf_op jit(solution)/shard_map/all_to_all | solution.py:40
  287.5 4.8 %copy-start.2 = (s32[16,4,128,128]{3,2,1,0:T(8,128)S(1)}, s32[16,4,128,128]{3,2,1,0:T(8,128)}, u32[]{:S(2)}) copy-start(s32[16,4,128,128]{3,2,1,0:T(8,128)} %param.8) | copy-start | bytes 12582916
  292.4 133.9 %copy-start.4 = (f32[16,128]{1,0:T(8,128)}, f32[16,128]{1,0:T(8,128)S(1)}, u32[]{:S(2)}) copy-start(f32[16,128]{1,0:T(8,128)S(1)} %get-tuple-element.18) | copy-start | bytes 24580
  305.2 12.2 %all-to-all-start.5 = ((f32[4,8,16,128]{3,2,0,1:T(8,128)}), f32[4,8,16,128]{3,2,0,1:T(8,128)S(1)}, u32[]{:S(2)}, u32[]{:S(2)}) async-start(f32[4,8,16,128]{3,2,0,1:T(8,128)} %copy.30), calls=%async_computation.5 | async-start | bytes 524288 | tf_op jit(solution)/shard_map/all_to_all | solution.py:40
where the time goes:
time: 427 us; the launch traced here: 426 us
  blocking collectives  346 us (81%)
  matrix products  23.5 us (6%)
  waiting for transfers between devices  19.7 us (5%)
  starting transfers between devices  12.7 us (3%)
  between operations  9.14 us (2%)
  other arithmetic  8.77 us (2%)
  local copies, waits for them, and re-layouts  6.74 us (2%)
    all_gather x3, blocking collectives, local(): mult = lax.all_gather(new_share, ('narrow', 'wide'), axis=0, tiled=True)  202 us
    psum x3, blocking collectives, local(): lax.psum((jnp.sum(slope * slope), jnp.sum(mult_share), local_soft), ('nar...  117 us
    all_to_all x3, blocking collectives, local(): lax.all_to_all(outgoing, 'narrow', split_axis=0, concat_axis=0, tiled=True)  26.8 us
    all_to_all x3, waiting for transfers between devices, local(): lax.all_to_all(lax.all_to_all(outgoing, 'narrow', split_axis=0, concat_ax...  19.7 us
    all_to_all x3, starting transfers between devices, local(): lax.all_to_all(lax.all_to_all(outgoing, 'narrow', split_axis=0, concat_ax...  12.7 us
    dot_general x3, matrix products, local(): reduced = costf - jnp.einsum('tkrc,tkr->tc', incf, u_tile, precision=hi)  12.3 us
    dot_general x3, matrix products, local(): jnp.einsum('tkrc,tc->tkr', incf, primal_mean, precision=hi)  10.2 us
  transfers between devices with their start and end apart: 3, of which 3 were waited for; matrix products, arithmetic and copies ran while one was open for 1% of the time, Pallas kernels for 0%

commit v1 on v0

--- a/solution.py
+++ b/solution.py
@@ -1,3 +1,4 @@
+import functools
 import jax
 import jax.numpy as jnp
 from jax import lax
@@ -6,6 +7,15 @@
 BLK = 128
 K = 4
 ITERS = 3
+
+
+def arrange_masks_in(incoming_x, row_axis, axis_key):
+    for dev_j in (row_axis, axis_key):
+        incoming_x = lax.psum(incoming_x, axis_name=dev_j)
+    return incoming_x
+
+
+shapes_settle = functools.partial(arrange_masks_in, row_axis="wide", axis_key="narrow")
 
 
 def local(block_ids, incidence, costs, start_mult, upper):
@@ -47,8 +57,8 @@
         cover_share = jnp.sum(jnp.sum(incoming, axis=0), axis=0)
         mult_share = lax.dynamic_slice_in_dim(mult, share_start, share_rows, 0)
         slope = 1.0 - cover_share
-        norm, mult_total, late_sum = lax.psum(
-            (jnp.sum(slope * slope), jnp.sum(mult_share), local_soft), ("narrow", "wide")
+        norm, mult_total, late_sum = shapes_settle(
+            (jnp.sum(slope * slope), jnp.sum(mult_share), local_soft)
         )
         value = mult_total + late_sum
         size = (upper[0] - value) / (norm + 1e-06)

time: 427 us -> 382 us (0.89)
  blocking collectives: 346 us -> 300 us
    psum x3 -> x6, blocking collectives: 117 us -> 79 us  [arrange_masks_in(): incoming_x = lax.psum(incoming_x, axis_name=dev_j)]
    all_gather x3, blocking collectives: 202 us -> 194 us  [local(): mult = lax.all_gather(new_share, ('narrow', 'wide'), axis=0, tiled=True)]
where the time goes in v1:
time: 382 us; the launch traced here: 381 us
  blocking collectives  300 us (79%)
  matrix products  23.5 us (6%)
  waiting for transfers between devices  19.5 us (5%)
  starting transfers between devices  13 us (3%)
  between operations  9.12 us (2%)
  other arithmetic  8.75 us (2%)
  local copies, waits for them, and re-layouts  6.74 us (2%)
    all_gather x3, blocking collectives, local(): mult = lax.all_gather(new_share, ('narrow', 'wide'), axis=0, tiled=True)  194 us
    psum x6, blocking collectives, arrange_masks_in(): incoming_x = lax.psum(incoming_x, axis_name=dev_j)  79 us
    all_to_all x3, blocking collectives, local(): lax.all_to_all(outgoing, 'narrow', split_axis=0, concat_axis=0, tiled=True)  26.8 us
    all_to_all x3, waiting for transfers between devices, local(): lax.all_to_all(lax.all_to_all(outgoing, 'narrow', split_axis=0, concat_ax...  19.5 us
    all_to_all x3, starting transfers between devices, local(): lax.all_to_all(lax.all_to_all(outgoing, 'narrow', split_axis=0, concat_ax...  13 us
    dot_general x3, matrix products, local(): reduced = costf - jnp.einsum('tkrc,tkr->tc', incf, u_tile, precision=hi)  12.3 us
    dot_general x3, matrix products, local(): jnp.einsum('tkrc,tc->tkr', incf, primal_mean, precision=hi)  10.2 us
  transfers between devices with their start and end apart: 3, of which 3 were waited for; matrix products, arithmetic and copies ran while one was open for 1% of the time, Pallas kernels for 0%

profile of v1, /device:TPU:0, one launch (start us, length us, event | category | flops | bytes accessed | tf_op | source)
XLA Modules:
  0.0 380.7 jit_solution(17048576300980439168)
XLA Ops:
  2.0 0.8 copy.23
  3.2 1.5 gather_fusion
  4.8 4.1 %fusion.10 = f32[16,1,128,1]{2,1,3,0:T(1,128)S(1)} fusion(f32[16,4,128,1]{2,3,1,0:T(1,128)S(1)} %bitcast.71, s32[16,4,128,128]{3,2,1,0:T(8,128)} %param.8), kind=kOutput, calls=%fused_computation.13 | convolution fusion | flops 13631488 | bytes 4235264 | tf_op jit(solution)/shard_map/tkrc,tkr->tc/dot_general | solution.py:38
  9.6 3.4 fusion.8
  13.3 10.0 %all_to_all.30 = f32[4,8,16,128]{3,2,1,0:T(8,128)S(1)} all-to-all(f32[4,8,16,128]{3,2,1,0:T(8,128)S(1)} %fusion.16), channel_id=1, replica_groups=mesh['narrow'=4,'wide'=8] {'narrow'}, dimensions={0} | all-to-all | bytes 524288 | tf_op jit(solution)/shard_map/all_to_all | solution.py:51
  23.3 0.7 copy.24
  24.1 5.8 %all-to-all-start.1 = ((f32[4,8,16,128]{3,2,0,1:T(8,128)}), f32[4,8,16,128]{3,2,0,1:T(8,128)S(1)}, u32[]{:S(2)}, u32[]{:S(2)}) async-start(f32[4,8,16,128]{3,2,0,1:T(8,128)} %copy.24), calls=%async_computation.1 | async-start | bytes 524288 | tf_op jit(solution)/shard_map/all_to_all | solution.py:50
  29.9 1.4 dynamic-slice_reduce_fusion.2
  32.6 5.8 %all-to-all-done.1 = f32[4,8,16,128]{3,2,0,1:T(8,128)S(1)} async-done(((f32[4,8,16,128]{3,2,0,1:T(8,128)}), f32[4,8,16,128]{3,2,0,1:T(8,128)S(1)}, u32[]{:S(2)}, u32[]{:S(2)}) %all-to-all-start.1) | async-done | bytes 262176 | tf_op jit(solution)/shard_map/all_to_all | solution.py:50
  39.7 20.1 %all-reduce.2 = (f32[]{:T(128)}, f32[]{:T(128)}) all-reduce(f32[]{:T(128)S(6)} %add.113, f32[]{:T(128)} %multiply_reduce_fusion.2), channel_id=1, replica_groups=mesh['narrow'=4,'wide'=8] {'wide'}, use_global_device_ids=true, to_apply=%region_1.2 | all-reduce | flops 2 | bytes 16 | tf_op jit(solution)/shard_map/psum | solution.py:14
  59.8 6.3 %all-reduce.5 = (f32[]{:T(128)}, f32[]{:T(128)}) all-reduce(f32[]{:T(128)} %get-tuple-element.7, f32[]{:T(128)} %get-tuple-element.8), channel_id=1, replica_groups=mesh['narrow'=4,'wide'=8] {'narrow'}, use_global_device_ids=true, to_apply=%region_2.3 | all-reduce | flops 2 | bytes 16 | tf_op jit(solution)/shard_map/psum | solution.py:14
  67.4 0.7 add_maximum_fusion.2
  68.1 64.7 %all_gather.9 = f32[512,128]{1,0:T(8,128)S(1)} all-gather(f32[16,128]{1,0:T(8,128)S(1)} %add_maximum_fusion.2), channel_id=1, replica_groups=mesh['narrow'=4,'wide'=8] {'narrow','wide'}, dimensions={0}, use_global_device_ids=true | all-gather | bytes 270336 | tf_op jit(solution)/shard_map/all_gather | solution.py:66
  133.5 4.1 %fusion.6 = f32[16,1,128,1]{2,1,3,0:T(1,128)S(1)} fusion(f32[16,4,128,1]{2,3,1,0:T(1,128)S(1)} %bitcast.72, s32[16,4,128,128]{3,2,1,0:T(8,128)} %param.8), kind=kOutput, calls=%fused_computation.9 | convolution fusion | flops 13631488 | bytes 4235264 | tf_op jit(solution)/shard_map/tkrc,tkr->tc/dot_general | solution.py:38
  138.3 3.4 fusion.4
  142.0 8.4 %all_to_all.31 = f32[4,8,16,128]{3,2,1,0:T(8,128)S(1)} all-to-all(f32[4,8,16,128]{3,2,1,0:T(8,128)S(1)} %fusion.14), channel_id=1, replica_groups=mesh['narrow'=4,'wide'=8] {'narrow'}, dimensions={0} | all-to-all | bytes 524288 | tf_op jit(solution)/shard_map/all_to_all | solution.py:51
  150.4 0.7 copy.27
  151.1 3.6 all-to-all-start.3
  156.5 6.8 %all-to-all-done.3 = f32[4,8,16,128]{3,2,0,1:T(8,128)S(1)} async-done(((f32[4,8,16,128]{3,2,0,1:T(8,128)}), f32[4,8,16,128]{3,2,0,1:T(8,128)S(1)}, u32[]{:S(2)}, u32[]{:S(2)}) %all-to-all-start.3) | async-done | bytes 262176 | tf_op jit(solution)/shard_map/all_to_all | solution.py:50
  164.0 20.1 %all-reduce.1 = (f32[]{:T(128)}, f32[]{:T(128)}) all-reduce(f32[]{:T(128)S(6)} %add.118, f32[]{:T(128)} %multiply_reduce_fusion.1), channel_id=1, replica_groups=mesh['narrow'=4,'wide'=8] {'wide'}, use_global_device_ids=true, to_apply=%region_11.13 | all-reduce | flops 2 | bytes 16 | tf_op jit(solution)/shard_map/psum | solution.py:14
  184.0 6.3 %all-reduce.4 = (f32[]{:T(128)}, f32[]{:T(128)}) all-reduce(f32[]{:T(128)} %get-tuple-element.5, f32[]{:T(128)} %get-tuple-element.6), channel_id=1, replica_groups=mesh['narrow'=4,'wide'=8] {'narrow'}, use_global_device_ids=true, to_apply=%region_12.14 | all-reduce | flops 2 | bytes 16 | tf_op jit(solution)/shard_map/psum | solution.py:14
  191.7 64.9 %all_gather.10 = f32[512,128]{1,0:T(8,128)S(1)} all-gather(f32[16,128]{1,0:T(8,128)S(1)} %add_maximum_fusion.1), channel_id=1, replica_groups=mesh['narrow'=4,'wide'=8] {'narrow','wide'}, dimensions={0}, use_global_device_ids=true | all-gather | bytes 270336 | tf_op jit(solution)/shard_map/all_gather | solution.py:66
  257.2 4.1 %fusion.2 = f32[16,1,128,1]{2,1,3,0:T(1,128)S(1)} fusion(f32[16,4,128,1]{2,3,1,0:T(1,128)S(1)} %bitcast.70, s32[16,4,128,128]{3,2,1,0:T(8,128)} %param.8), kind=kOutput, calls=%fused_computation.5 | convolution fusion | flops 13631488 | bytes 4235264 | tf_op jit(solution)/shard_map/tkrc,tkr->tc/dot_general | solution.py:38
  262.0 3.4 fusion
  265.7 8.4 %all_to_all.32 = f32[4,8,16,128]{3,2,1,0:T(8,128)S(1)} all-to-all(f32[4,8,16,128]{3,2,1,0:T(8,128)S(1)} %fusion.12), channel_id=1, replica_groups=mesh['narrow'=4,'wide'=8] {'narrow'}, dimensions={0} | all-to-all | bytes 524288 | tf_op jit(solution)/shard_map/all_to_all | solution.py:51
  274.1 0.7 copy.30
  274.8 3.6 all-to-all-start.5
  280.2 6.8 %all-to-all-done.5 = f32[4,8,16,128]{3,2,0,1:T(8,128)S(1)} async-done(((f32[4,8,16,128]{3,2,0,1:T(8,128)}), f32[4,8,16,128]{3,2,0,1:T(8,128)S(1)}, u32[]{:S(2)}, u32[]{:S(2)}) %all-to-all-start.5) | async-done | bytes 262176 | tf_op jit(solution)/shard_map/all_to_all | solution.py:50
  287.7 20.1 %all-reduce = (f32[]{:T(128)}, f32[]{:T(128)}) all-reduce(f32[]{:T(128)S(6)} %add.124, f32[]{:T(128)} %multiply_reduce_fusion), channel_id=1, replica_groups=mesh['narrow'=4,'wide'=8] {'wide'}, use_global_device_ids=true, to_apply=%region_21.23 | all-reduce | flops 2 | bytes 16 | tf_op jit(solution)/shard_map/psum | solution.py:14
  307.8 6.3 %all-reduce.3 = (f32[]{:T(128)}, f32[]{:T(128)}) all-reduce(f32[]{:T(128)} %get-tuple-element.3, f32[]{:T(128)} %get-tuple-element.4), channel_id=1, replica_groups=mesh['narrow'=4,'wide'=8] {'narrow'}, use_global_device_ids=true, to_apply=%region_22.24 | all-reduce | flops 2 | bytes 16 | tf_op jit(solution)/shard_map/psum | solution.py:14
  315.3 64.7 %all_gather.11 = f32[512,128]{1,0:T(8,128)S(1)} all-gather(f32[16,128]{1,0:T(8,128)S(1)} %add_maximum_fusion), channel_id=1, replica_groups=mesh['narrow'=4,'wide'=8] {'narrow','wide'}, dimensions={0}, use_global_device_ids=true | all-gather | bytes 270336 | tf_op jit(solution)/shard_map/all_gather | solution.py:66
  380.0 0.7 copy.48
  (39 shorter events, 9.2 us)
Async XLA Ops:
  0.6 8.3 %copy-start.3 = (s32[16,128]{1,0:T(8,128)S(1)}, s32[16,128]{1,0:T(8,128)}, u32[]{:S(2)}) copy-start(s32[16,128]{1,0:T(8,128)} %param.9) | copy-start | bytes 24580
  4.7 4.9 %copy-start = (s32[16,4,128,128]{3,2,1,0:T(8,128)S(1)}, s32[16,4,128,128]{3,2,1,0:T(8,128)}, u32[]{:S(2)}) copy-start(s32[16,4,128,128]{3,2,1,0:T(8,128)} %param.8) | copy-start | bytes 12582916
  24.1 14.4 %all-to-all-start.1 = ((f32[4,8,16,128]{3,2,0,1:T(8,128)}), f32[4,8,16,128]{3,2,0,1:T(8,128)S(1)}, u32[]{:S(2)}, u32[]{:S(2)}) async-start(f32[4,8,16,128]{3,2,0,1:T(8,128)} %copy.24), calls=%async_computation.1 | async-start | bytes 524288 | tf_op jit(solution)/shard_map/all_to_all | solution.py:50
  133.4 4.8 %copy-start.1 = (s32[16,4,128,128]{3,2,1,0:T(8,128)S(1)}, s32[16,4,128,128]{3,2,1,0:T(8,128)}, u32[]{:S(2)}) copy-start(s32[16,4,128,128]{3,2,1,0:T(8,128)} %param.8) | copy-start | bytes 12582916
  151.1 12.2 %all-to-all-start.3 = ((f32[4,8,16,128]{3,2,0,1:T(8,128)}), f32[4,8,16,128]{3,2,0,1:T(8,128)S(1)}, u32[]{:S(2)}, u32[]{:S(2)}) async-start(f32[4,8,16,128]{3,2,0,1:T(8,128)} %copy.27), calls=%async_computation.3 | async-start | bytes 524288 | tf_op jit(solution)/shard_map/all_to_all | solution.py:50
  257.2 4.8 %copy-start.2 = (s32[16,4,128,128]{3,2,1,0:T(8,128)S(1)}, s32[16,4,128,128]{3,2,1,0:T(8,128)}, u32[]{:S(2)}) copy-start(s32[16,4,128,128]{3,2,1,0:T(8,128)} %param.8) | copy-start | bytes 12582916
  262.0 118.7 %copy-start.4 = (f32[16,128]{1,0:T(8,128)}, f32[16,128]{1,0:T(8,128)S(1)}, u32[]{:S(2)}) copy-start(f32[16,128]{1,0:T(8,128)S(1)} %get-tuple-element.24) | copy-start | bytes 24580
  274.8 12.2 %all-to-all-start.5 = ((f32[4,8,16,128]{3,2,0,1:T(8,128)}), f32[4,8,16,128]{3,2,0,1:T(8,128)S(1)}, u32[]{:S(2)}, u32[]{:S(2)}) async-start(f32[4,8,16,128]{3,2,0,1:T(8,128)} %copy.30), calls=%async_computation.5 | async-start | bytes 524288 | tf_op jit(solution)/shard_map/all_to_all | solution.py:50
